TPU v7x, 32 devices: a whole 2x2x4 slice. The times are simulated.
32 devices in a mesh: groups: 2 (over y), rows: 4 (over z), cols: 2 (over x), sub: 2 (over core).
Axes of the slice: x: 2, y: 2, z: 4, core: 2. Of those that a mesh axis runs over, the one named last changes fastest.
Arguments:
- returns: float32 [8, 64, 8192], P('groups', 'rows', ('cols', 'sub')), parts along dimension 0, may hold values from -6 to 6
- starts: int32 [8, 8192], P('groups', ('cols', 'sub')), parts along dimension 0, may hold values from 0 to 32
- start_block: float32 [8, 32, 8192], P('groups', None, ('cols', 'sub')), parts along dimension 0, may hold values from -6 to 6
Outputs:
- loadings: float32 [8, 32, 8192], P('groups', None, ('cols', 'sub')), parts along dimension 0
There are 2 independent parts, one for each index of `groups`. A program takes and returns all parts, laid end to end along the dimension named above; each array names one. Nothing has to cross between parts.
Inputs may be any that keep to these rules, and one draw needn't show every extreme that they name: `starts`: days before an asset's start day hold returns that do not count.
All inputs are finite; a program needn't handle non-finite values.
Results may differ from a plain program's by a relative error of at most 0.0078.
Values may be sent and summed in bfloat16 or wider, within the bound.
A program may use at most 64 MiB of HBM per device.

v0:
```python
import jax
import jax.numpy as jnp
from jax import lax
from jax.sharding import PartitionSpec as P

ASSETS = 8192
ITERS = 3


def gram_of(image):
    return jnp.einsum("wkj,wlj->wkl", image, image, precision=lax.Precision.HIGHEST)


def project(factors, scaled):
    rounded = factors.astype(jnp.bfloat16)
    return jnp.einsum("wka,wta->wkt", rounded, scaled, preferred_element_type=jnp.float32)


def expand(proj, widened):
    return jnp.einsum("wkt,wta->wka", proj, widened, precision=lax.Precision.HIGHEST)


def orthonormal(image, gram):
    lower = jnp.linalg.cholesky(gram / ASSETS)
    return jax.scipy.linalg.solve_triangular(lower, image, lower=True)


def on_device(returns, starts, start_block):
    windows, days, width = returns.shape
    rows_count = lax.axis_size("rows")
    row_pos = lax.axis_index("rows")
    total_days = days * rows_count
    day_index = row_pos * days + jnp.arange(days, dtype=jnp.int32)
    live = (day_index[None, :, None] >= starts[:, None, :]).astype(jnp.float32)
    counts = (total_days - starts).astype(jnp.float32)
    masked = live * returns
    sums = lax.psum(jnp.sum(masked, axis=1), "rows")
    mean = sums / counts
    centered = live * (returns - mean[:, None, :])
    squares = lax.psum(jnp.sum(centered * centered, axis=1), "rows")
    scaled = (centered * lax.rsqrt(squares + 1.0)[:, None, :]).astype(jnp.bfloat16)
    widened = scaled.astype(jnp.float32)
    factors = start_block
    for step in range(ITERS):
        proj = lax.psum(project(factors, scaled), ("cols", "sub"))
        image = lax.psum(expand(proj, widened), "rows")
        gram = lax.psum(gram_of(image), ("cols", "sub"))
        factors = orthonormal(image, gram)
    return factors


def solution(mesh):
    placed = (
        P("groups", "rows", ("cols", "sub")),
        P("groups", ("cols", "sub")),
        P("groups", None, ("cols", "sub")),
    )
    return jax.shard_map(
        on_device,
        mesh=mesh,
        in_specs=placed,
        out_specs=P("groups", None, ("cols", "sub")),
        check_vma=False,
    )
```

profile of v0, /device:TPU:0, one launch (start us, length us, event | category | flops | bytes accessed | tf_op | source)
XLA Modules:
  0.0 354.8 jit_solution(6312155068273593770)
XLA Ops:
  6.5 1.3 fusion
  7.9 20.9 %psum.77 = f32[4,2048]{1,0:T(4,128)S(1)} all-reduce(f32[4,2048]{1,0:T(4,128)S(1)} %fusion), channel_id=1, replica_groups=mesh['groups'=2,'rows'=4,'cols'=2,'sub'=2] {'rows'}, use_global_device_ids=true, to_apply=%region_1.0 | all-reduce | flops 8192 | bytes 65536 | tf_op jit(solution)/shard_map/psum | solution.py:37
  28.9 0.2 multiply_reduce_fusion
  29.1 15.8 %psum.78 = f32[4,2048]{1,0:T(4,128)S(1)} all-reduce(f32[4,2048]{1,0:T(4,128)S(1)} %multiply_reduce_fusion), channel_id=1, replica_groups=mesh['groups'=2,'rows'=4,'cols'=2,'sub'=2] {'rows'}, use_global_device_ids=true, to_apply=%region_3.0 | all-reduce | flops 8192 | bytes 65536 | tf_op jit(solution)/shard_map/psum | solution.py:40
  44.9 0.2 multiply_convert_fusion
  45.1 0.2 convolution_bitcast_fusion
  45.3 10.3 %psum.79 = f32[4,32,16]{1,2,0:T(8,128)S(1)} all-reduce(f32[4,32,16]{1,2,0:T(8,128)S(1)} %convolution_bitcast_fusion), channel_id=1, replica_groups=mesh['groups'=2,'rows'=4,'cols'=2,'sub'=2] {'cols','sub'}, use_global_device_ids=true, to_apply=%region_4.0 | all-reduce | flops 2048 | bytes 16384 | tf_op jit(solution)/shard_map/psum | solution.py:45
  55.6 1.6 fusion.9
  57.3 51.6 %all-reduce.4.cloned.1.call-done = f32[4,32,2048]{2,1,0:T(8,128)} async-done(((f32[4,32,2048]{2,1,0:T(8,128)}), f32[4,32,2048]{2,1,0:T(8,128)}) %all-reduce.4.cloned.1.call-update) | async-done | bytes 1048592 | tf_op jit(solution)/shard_map/psum | solution.py:46
  108.8 2.7 fusion.10
  111.6 11.8 %psum.81 = f32[4,32,32]{1,2,0:T(8,128)S(1)} all-reduce(f32[4,32,32]{1,2,0:T(8,128)S(1)} %fusion.10), channel_id=1, replica_groups=mesh['groups'=2,'rows'=4,'cols'=2,'sub'=2] {'cols','sub'}, use_global_device_ids=true, to_apply=%region_6.0 | all-reduce | flops 4096 | bytes 32768 | tf_op jit(solution)/shard_map/psum | solution.py:47
  123.6 11.7 %custom-call.10 = f32[4,32,32]{2,1,0:T(8,128)S(1)} custom-call(f32[4,32,32]{2,1,0:T(8,128)S(1)} %fusion.8), custom_call_target="Cholesky" | custom-call | tf_op jit(solution)/shard_map/jit(cholesky)/cholesky | solution.py:24
  135.5 9.8 %custom-call.11 = f32[4,1,32,32]{2,3,1,0:T(8,128)S(1)} custom-call(f32[4,1,32,32]{3,2,1,0:T(8,128)S(1)} %select_bitcast_fusion.2), custom_call_target="InvertDiagBlocksLowerTriangular" | custom-call | tf_op jit(solution)/shard_map/jit(_solve_triangular)/vmap()/triangular_solve | solution.py:25
  145.4 1.1 convolution_convert_fusion.1
  146.4 0.2 fusion.11
  146.7 10.5 %psum.82 = f32[4,32,16]{1,2,0:T(8,128)S(1)} all-reduce(f32[4,32,16]{1,2,0:T(8,128)S(1)} %fusion.11), channel_id=1, replica_groups=mesh['groups'=2,'rows'=4,'cols'=2,'sub'=2] {'cols','sub'}, use_global_device_ids=true, to_apply=%region_9.0 | all-reduce | flops 2048 | bytes 16384 | tf_op jit(solution)/shard_map/psum | solution.py:45
  157.2 1.6 fusion.12
  158.8 50.5 %all-reduce.6.cloned.1.call-done = f32[4,32,2048]{2,1,0:T(8,128)} async-done(((f32[4,32,2048]{2,1,0:T(8,128)}), f32[4,32,2048]{2,1,0:T(8,128)}) %all-reduce.6.cloned.1.call-update) | async-done | bytes 1048592 | tf_op jit(solution)/shard_map/psum | solution.py:46
  209.3 2.7 fusion.13
  212.0 11.8 %psum.84 = f32[4,32,32]{1,2,0:T(8,128)S(1)} all-reduce(f32[4,32,32]{1,2,0:T(8,128)S(1)} %fusion.13), channel_id=1, replica_groups=mesh['groups'=2,'rows'=4,'cols'=2,'sub'=2] {'cols','sub'}, use_global_device_ids=true, to_apply=%region_11.0 | all-reduce | flops 4096 | bytes 32768 | tf_op jit(solution)/shard_map/psum | solution.py:47
  224.0 11.7 %custom-call.12 = f32[4,32,32]{2,1,0:T(8,128)S(1)} custom-call(f32[4,32,32]{2,1,0:T(8,128)S(1)} %fusion.6), custom_call_target="Cholesky" | custom-call | tf_op jit(solution)/shard_map/jit(cholesky)/cholesky | solution.py:24
  236.0 9.8 %custom-call.13 = f32[4,1,32,32]{2,3,1,0:T(8,128)S(1)} custom-call(f32[4,1,32,32]{3,2,1,0:T(8,128)S(1)} %select_bitcast_fusion.1), custom_call_target="InvertDiagBlocksLowerTriangular" | custom-call | tf_op jit(solution)/shard_map/jit(_solve_triangular)/vmap()/triangular_solve | solution.py:25
  245.8 1.1 convolution_convert_fusion
  246.9 0.2 fusion.14
  247.1 10.5 %psum.85 = f32[4,32,16]{1,2,0:T(8,128)S(1)} all-reduce(f32[4,32,16]{1,2,0:T(8,128)S(1)} %fusion.14), channel_id=1, replica_groups=mesh['groups'=2,'rows'=4,'cols'=2,'sub'=2] {'cols','sub'}, use_global_device_ids=true, to_apply=%region_12.0 | all-reduce | flops 2048 | bytes 16384 | tf_op jit(solution)/shard_map/psum | solution.py:45
  257.6 1.6 fusion.15
  259.2 50.5 %all-reduce.8.cloned.1.call-done = f32[4,32,2048]{2,1,0:T(8,128)} async-done(((f32[4,32,2048]{2,1,0:T(8,128)}), f32[4,32,2048]{2,1,0:T(8,128)}) %all-reduce.8.cloned.1.call-update) | async-done | bytes 1048592 | tf_op jit(solution)/shard_map/psum | solution.py:46
  309.7 2.7 fusion.16
  312.5 11.8 %psum.87 = f32[4,32,32]{1,2,0:T(8,128)S(1)} all-reduce(f32[4,32,32]{1,2,0:T(8,128)S(1)} %fusion.16), channel_id=1, replica_groups=mesh['groups'=2,'rows'=4,'cols'=2,'sub'=2] {'cols','sub'}, use_global_device_ids=true, to_apply=%region_14.17 | all-reduce | flops 4096 | bytes 32768 | tf_op jit(solution)/shard_map/psum | solution.py:47
  324.5 11.7 %custom-call.14 = f32[4,32,32]{2,1,0:T(8,128)S(1)} custom-call(f32[4,32,32]{2,1,0:T(8,128)S(1)} %fusion.4), custom_call_target="Cholesky" | custom-call | tf_op jit(solution)/shard_map/jit(cholesky)/cholesky | solution.py:24
  336.4 9.8 %custom-call.15 = f32[4,1,32,32]{2,3,1,0:T(8,128)S(1)} custom-call(f32[4,1,32,32]{3,2,1,0:T(8,128)S(1)} %select_bitcast_fusion), custom_call_target="InvertDiagBlocksLowerTriangular" | custom-call | tf_op jit(solution)/shard_map/jit(_solve_triangular)/vmap()/triangular_solve | solution.py:25
  346.3 2.0 fusion.2
  (41 shorter events, 1.2 us)
Async XLA Ops:
  6.5 22.3 %copy-start.3 = (f32[4,16,2048]{2,1,0:T(8,128)S(1)}, f32[4,16,2048]{2,1,0:T(8,128)}, u32[]{:S(2)}) copy-start(f32[4,16,2048]{2,1,0:T(8,128)} %param.6) | copy-start | bytes 1572868
  6.5 102.3 %all-reduce.4.cloned.1.call-start = ((), (), s32[]{:S(2)}) async-start(), calls=%async_computation | async-start | bytes 2097152 | tf_op jit(solution)/shard_map/psum | solution.py:46
  6.5 22.3 %copy-start.5 = (s32[4,2048]{1,0:T(4,128)S(1)}, s32[4,2048]{1,0:T(4,128)}, u32[]{:S(2)}) copy-start(s32[4,2048]{1,0:T(4,128)} %param.7) | copy-start | bytes 98308
  7.8 37.2 %copy-start.4 = (f32[4,32,2048]{2,1,0:T(8,128)S(1)}, f32[4,32,2048]{2,1,0:T(8,128)}, u32[]{:S(2)}) copy-start(f32[4,32,2048]{2,1,0:T(8,128)} %param.8) | copy-start | bytes 3145732
  57.2 152.1 %all-reduce.6.cloned.1.call-start = ((), (), s32[]{:S(2)}) async-start(), calls=%async_computation.1 | async-start | bytes 2097152 | tf_op jit(solution)/shard_map/psum | solution.py:46
  108.8 36.5 %copy-start = (f32[4,32,2048]{2,1,0:T(8,128)S(1)}, f32[4,32,2048]{2,1,0:T(8,128)}, u32[]{:S(2)}) copy-start(f32[4,32,2048]{2,1,0:T(8,128)} %all-reduce.4.cloned.1.call-done) | copy-start | bytes 3145732
  158.8 151.0 %all-reduce.8.cloned.1.call-start = ((), (), s32[]{:S(2)}) async-start(), calls=%async_computation.2 | async-start | bytes 2097152 | tf_op jit(solution)/shard_map/psum | solution.py:46
  209.3 36.5 %copy-start.1 = (f32[4,32,2048]{2,1,0:T(8,128)S(1)}, f32[4,32,2048]{2,1,0:T(8,128)}, u32[]{:S(2)}) copy-start(f32[4,32,2048]{2,1,0:T(8,128)} %all-reduce.6.cloned.1.call-done) | copy-start | bytes 3145732
  309.7 36.5 %copy-start.2 = (f32[4,32,2048]{2,1,0:T(8,128)S(1)}, f32[4,32,2048]{2,1,0:T(8,128)}, u32[]{:S(2)}) copy-start(f32[4,32,2048]{2,1,0:T(8,128)} %all-reduce.8.cloned.1.call-done) | copy-start | bytes 3145732
Sparse Core Ops, SparseCore 0:
  57.3 51.4 all-reduce.3
  158.9 50.3 all-reduce.5
  259.3 50.3 all-reduce.7
where the time goes:
time: 355 us
  waiting for transfers between devices  153 us (43%)
  blocking collectives  103 us (29%)
  other arithmetic  67.2 us (19%)
  matrix products  17.9 us (5%)
  between operations  13.4 us (4%)
    psum x3, waiting for transfers between devices, on_device(): image = lax.psum(expand(proj, widened), 'rows')  153 us
    another operation x10, other arithmetic, orthonormal(): lower = jnp.linalg.cholesky(gram / ASSETS)  35.6 us
    psum x3, blocking collectives, on_device(): gram = lax.psum(gram_of(image), ('cols', 'sub'))  35.5 us
    psum x3, blocking collectives, on_device(): proj = lax.psum(project(factors, scaled), ('cols', 'sub'))  31.2 us
    another operation x7, other arithmetic, orthonormal(): return jax.scipy.linalg.solve_triangular(lower, image, lower=True)  29.8 us
    psum x1, blocking collectives, on_device(): sums = lax.psum(jnp.sum(masked, axis=1), 'rows')  20.9 us
    psum x1, blocking collectives, on_device(): squares = lax.psum(jnp.sum(centered * centered, axis=1), 'rows')  15.8 us
    dot_general x3, matrix products, gram_of(): jnp.einsum('wkj,wlj->wkl', image, image, precision=lax.Precision.HIGHEST)  8.19 us
  transfers between devices with their start and end apart: 3, of which 3 were waited for; matrix products, arithmetic and copies ran while one was open for 0% of the time, Pallas kernels for 0%

commit v1 on v0

--- a/solution.py
+++ b/solution.py
@@ -42,7 +42,7 @@
     widened = scaled.astype(jnp.float32)
     factors = start_block
     for step in range(ITERS):
-        proj = lax.psum(project(factors, scaled), ("cols", "sub"))
+        proj = lax.psum(lax.psum(project(factors, scaled), "sub"), "cols")
         image = lax.psum(expand(proj, widened), "rows")
         gram = lax.psum(gram_of(image), ("cols", "sub"))
         factors = orthonormal(image, gram)

time: 355 us -> 358 us (level)
    psum x3 -> x6, blocking collectives: 31.2 us -> 33.5 us  [on_device(): proj = lax.psum(lax.psum(project(factors, scaled), 'sub'), 'cols')]
where the time goes in v1:
time: 358 us
  waiting for transfers between devices  153 us (43%)
  blocking collectives  106 us (30%)
  other arithmetic  67.2 us (19%)
  matrix products  17.9 us (5%)
  between operations  13.4 us (4%)
    psum x3, waiting for transfers between devices, on_device(): image = lax.psum(expand(proj, widened), 'rows')  153 us
    another operation x10, other arithmetic, orthonormal(): lower = jnp.linalg.cholesky(gram / ASSETS)  35.6 us
    psum x3, blocking collectives, on_device(): gram = lax.psum(gram_of(image), ('cols', 'sub'))  35.5 us
    psum x6, blocking collectives, on_device(): proj = lax.psum(lax.psum(project(factors, scaled), 'sub'), 'cols')  33.5 us
    another operation x7, other arithmetic, orthonormal(): return jax.scipy.linalg.solve_triangular(lower, image, lower=True)  29.8 us
    psum x1, blocking collectives, on_device(): sums = lax.psum(jnp.sum(masked, axis=1), 'rows')  20.9 us
    psum x1, blocking collectives, on_device(): squares = lax.psum(jnp.sum(centered * centered, axis=1), 'rows')  15.8 us
    dot_general x3, matrix products, gram_of(): jnp.einsum('wkj,wlj->wkl', image, image, precision=lax.Precision.HIGHEST)  8.19 us
  transfers between devices with their start and end apart: 3, of which 3 were waited for; matrix products, arithmetic and copies ran while one was open for 0% of the time, Pallas kernels for 0%

profile of v1, /device:TPU:0, one launch (start us, length us, event | category | flops | bytes accessed | tf_op | source)
XLA Modules:
  0.0 357.5 jit_solution(3543521484816449294)
XLA Ops:
  6.5 1.3 fusion
  7.9 20.9 %psum.98 = f32[4,2048]{1,0:T(4,128)S(1)} all-reduce(f32[4,2048]{1,0:T(4,128)S(1)} %fusion), channel_id=1, replica_groups=mesh['groups'=2,'rows'=4,'cols'=2,'sub'=2] {'rows'}, use_global_device_ids=true, to_apply=%region_1.0 | all-reduce | flops 8192 | bytes 65536 | tf_op jit(solution)/shard_map/psum | solution.py:37
  29.1 15.8 %psum.99 = f32[4,2048]{1,0:T(4,128)S(1)} all-reduce(f32[4,2048]{1,0:T(4,128)S(1)} %multiply_reduce_fusion), channel_id=1, replica_groups=mesh['groups'=2,'rows'=4,'cols'=2,'sub'=2] {'rows'}, use_global_device_ids=true, to_apply=%region_3.0 | all-reduce | flops 8192 | bytes 65536 | tf_op jit(solution)/shard_map/psum | solution.py:40
  45.1 0.2 convolution_bitcast_fusion
  45.3 3.4 psum.100
  48.7 8.3 %psum.101 = f32[4,32,16]{1,2,0:T(8,128)S(1)} all-reduce(f32[4,32,16]{1,2,0:T(8,128)S(1)} %psum.100), channel_id=1, replica_groups=mesh['groups'=2,'rows'=4,'cols'=2,'sub'=2] {'cols'}, use_global_device_ids=true, to_apply=%region_5.0 | all-reduce | flops 2048 | bytes 16384 | tf_op jit(solution)/shard_map/psum | solution.py:45
  57.1 1.6 fusion.9
  58.8 50.5 %all-reduce.4.cloned.1.call-done = f32[4,32,2048]{2,1,0:T(8,128)} async-done(((f32[4,32,2048]{2,1,0:T(8,128)}), f32[4,32,2048]{2,1,0:T(8,128)}) %all-reduce.4.cloned.1.call-update) | async-done | bytes 1048592 | tf_op jit(solution)/shard_map/psum | solution.py:46
  109.3 2.7 fusion.10
  112.0 11.8 %psum.103 = f32[4,32,32]{1,2,0:T(8,128)S(1)} all-reduce(f32[4,32,32]{1,2,0:T(8,128)S(1)} %fusion.10), channel_id=1, replica_groups=mesh['groups'=2,'rows'=4,'cols'=2,'sub'=2] {'cols','sub'}, use_global_device_ids=true, to_apply=%region_7.0 | all-reduce | flops 4096 | bytes 32768 | tf_op jit(solution)/shard_map/psum | solution.py:47
  124.0 11.7 %custom-call.10 = f32[4,32,32]{2,1,0:T(8,128)S(1)} custom-call(f32[4,32,32]{2,1,0:T(8,128)S(1)} %fusion.8), custom_call_target="Cholesky" | custom-call | tf_op jit(solution)/shard_map/jit(cholesky)/cholesky | solution.py:24
  136.0 9.8 %custom-call.11 = f32[4,1,32,32]{2,3,1,0:T(8,128)S(1)} custom-call(f32[4,1,32,32]{3,2,1,0:T(8,128)S(1)} %select_bitcast_fusion.2), custom_call_target="InvertDiagBlocksLowerTriangular" | custom-call | tf_op jit(solution)/shard_map/jit(_solve_triangular)/vmap()/triangular_solve | solution.py:25
  145.8 1.1 convolution_convert_fusion.1
  146.9 0.2 fusion.11
  147.1 3.4 psum.104
  150.6 7.4 %psum.105 = f32[4,32,16]{1,2,0:T(8,128)S(1)} all-reduce(f32[4,32,16]{1,2,0:T(8,128)S(1)} %psum.104), channel_id=1, replica_groups=mesh['groups'=2,'rows'=4,'cols'=2,'sub'=2] {'cols'}, use_global_device_ids=true, to_apply=%region_11.0 | all-reduce | flops 2048 | bytes 16384 | tf_op jit(solution)/shard_map/psum | solution.py:45
  158.0 1.6 fusion.12
  159.7 51.2 %all-reduce.6.cloned.1.call-done = f32[4,32,2048]{2,1,0:T(8,128)} async-done(((f32[4,32,2048]{2,1,0:T(8,128)}), f32[4,32,2048]{2,1,0:T(8,128)}) %all-reduce.6.cloned.1.call-update) | async-done | bytes 1048592 | tf_op jit(solution)/shard_map/psum | solution.py:46
  210.9 2.7 fusion.13
  213.6 11.8 %psum.107 = f32[4,32,32]{1,2,0:T(8,128)S(1)} all-reduce(f32[4,32,32]{1,2,0:T(8,128)S(1)} %fusion.13), channel_id=1, replica_groups=mesh['groups'=2,'rows'=4,'cols'=2,'sub'=2] {'cols','sub'}, use_global_device_ids=true, to_apply=%region_13.0 | all-reduce | flops 4096 | bytes 32768 | tf_op jit(solution)/shard_map/psum | solution.py:47
  225.6 11.7 %custom-call.12 = f32[4,32,32]{2,1,0:T(8,128)S(1)} custom-call(f32[4,32,32]{2,1,0:T(8,128)S(1)} %fusion.6), custom_call_target="Cholesky" | custom-call | tf_op jit(solution)/shard_map/jit(cholesky)/cholesky | solution.py:24
  237.5 9.8 %custom-call.13 = f32[4,1,32,32]{2,3,1,0:T(8,128)S(1)} custom-call(f32[4,1,32,32]{3,2,1,0:T(8,128)S(1)} %select_bitcast_fusion.1), custom_call_target="InvertDiagBlocksLowerTriangular" | custom-call | tf_op jit(solution)/shard_map/jit(_solve_triangular)/vmap()/triangular_solve | solution.py:25
  247.4 1.1 convolution_convert_fusion
  248.7 3.4 psum.108
  252.1 7.5 %psum.109 = f32[4,32,16]{1,2,0:T(8,128)S(1)} all-reduce(f32[4,32,16]{1,2,0:T(8,128)S(1)} %psum.108), channel_id=1, replica_groups=mesh['groups'=2,'rows'=4,'cols'=2,'sub'=2] {'cols'}, use_global_device_ids=true, to_apply=%region_15.0 | all-reduce | flops 2048 | bytes 16384 | tf_op jit(solution)/shard_map/psum | solution.py:45
  259.6 1.6 fusion.15
  261.2 51.2 %all-reduce.8.cloned.1.call-done = f32[4,32,2048]{2,1,0:T(8,128)} async-done(((f32[4,32,2048]{2,1,0:T(8,128)}), f32[4,32,2048]{2,1,0:T(8,128)}) %all-reduce.8.cloned.1.call-update) | async-done | bytes 1048592 | tf_op jit(solution)/shard_map/psum | solution.py:46
  312.5 2.7 fusion.16
  315.2 11.8 %psum.111 = f32[4,32,32]{1,2,0:T(8,128)S(1)} all-reduce(f32[4,32,32]{1,2,0:T(8,128)S(1)} %fusion.16), channel_id=1, replica_groups=mesh['groups'=2,'rows'=4,'cols'=2,'sub'=2] {'cols','sub'}, use_global_device_ids=true, to_apply=%region_17.20 | all-reduce | flops 4096 | bytes 32768 | tf_op jit(solution)/shard_map/psum | solution.py:47
  327.2 11.7 %custom-call.14 = f32[4,32,32]{2,1,0:T(8,128)S(1)} custom-call(f32[4,32,32]{2,1,0:T(8,128)S(1)} %fusion.4), custom_call_target="Cholesky" | custom-call | tf_op jit(solution)/shard_map/jit(cholesky)/cholesky | solution.py:24
  339.1 9.8 %custom-call.15 = f32[4,1,32,32]{2,3,1,0:T(8,128)S(1)} custom-call(f32[4,1,32,32]{3,2,1,0:T(8,128)S(1)} %select_bitcast_fusion), custom_call_target="InvertDiagBlocksLowerTriangular" | custom-call | tf_op jit(solution)/shard_map/jit(_solve_triangular)/vmap()/triangular_solve | solution.py:25
  349.0 2.0 fusion.2
  (44 shorter events, 1.8 us)
Async XLA Ops:
  6.5 22.3 %copy-start.3 = (f32[4,16,2048]{2,1,0:T(8,128)S(1)}, f32[4,16,2048]{2,1,0:T(8,128)}, u32[]{:S(2)}) copy-start(f32[4,16,2048]{2,1,0:T(8,128)} %param.6) | copy-start | bytes 1572868
  6.5 102.8 %all-reduce.4.cloned.1.call-start = ((), (), s32[]{:S(2)}) async-start(), calls=%async_computation | async-start | bytes 2097152 | tf_op jit(solution)/shard_map/psum | solution.py:46
  6.5 22.3 %copy-start.5 = (s32[4,2048]{1,0:T(4,128)S(1)}, s32[4,2048]{1,0:T(4,128)}, u32[]{:S(2)}) copy-start(s32[4,2048]{1,0:T(4,128)} %param.7) | copy-start | bytes 98308
  7.8 37.2 %copy-start.4 = (f32[4,32,2048]{2,1,0:T(8,128)S(1)}, f32[4,32,2048]{2,1,0:T(8,128)}, u32[]{:S(2)}) copy-start(f32[4,32,2048]{2,1,0:T(8,128)} %param.8) | copy-start | bytes 3145732
  58.7 152.2 %all-reduce.6.cloned.1.call-start = ((), (), s32[]{:S(2)}) async-start(), calls=%async_computation.1 | async-start | bytes 2097152 | tf_op jit(solution)/shard_map/psum | solution.py:46
  109.3 36.5 %copy-start = (f32[4,32,2048]{2,1,0:T(8,128)S(1)}, f32[4,32,2048]{2,1,0:T(8,128)}, u32[]{:S(2)}) copy-start(f32[4,32,2048]{2,1,0:T(8,128)} %all-reduce.4.cloned.1.call-done) | copy-start | bytes 3145732
  159.6 152.8 %all-reduce.8.cloned.1.call-start = ((), (), s32[]{:S(2)}) async-start(), calls=%async_computation.2 | async-start | bytes 2097152 | tf_op jit(solution)/shard_map/psum | solution.py:46
  210.9 36.5 %copy-start.1 = (f32[4,32,2048]{2,1,0:T(8,128)S(1)}, f32[4,32,2048]{2,1,0:T(8,128)}, u32[]{:S(2)}) copy-start(f32[4,32,2048]{2,1,0:T(8,128)} %all-reduce.6.cloned.1.call-done) | copy-start | bytes 3145732
  312.4 36.5 %copy-start.2 = (f32[4,32,2048]{2,1,0:T(8,128)S(1)}, f32[4,32,2048]{2,1,0:T(8,128)}, u32[]{:S(2)}) copy-start(f32[4,32,2048]{2,1,0:T(8,128)} %all-reduce.8.cloned.1.call-done) | copy-start | bytes 3145732
Sparse Core Ops, SparseCore 0:
  58.8 50.4 all-reduce.3
  159.7 51.0 all-reduce.5
  261.3 51.0 all-reduce.7
